TPU v7x, 32 devices: a whole 2x2x4 slice. The times are simulated.
32 devices in a mesh: grp: 4 (over y, x), sub: 8 (over z, core).
Axes of the slice: x: 2, y: 2, z: 4, core: 2. Of those that a mesh axis runs over, the one named last changes fastest.
Arguments:
- initial_field: float32 [4, 16, 16384], P('grp', 'sub'), may hold values from -6 to 6
- conduct: float32 [4, 16, 16384], P('grp', 'sub'), may hold values from 0.02 to 0.12
- velocity: float32 [4, 16, 16384], P('grp', 'sub'), may hold values from 0 to 0.25
- heat_release: float32 [4, 16, 16384], P('grp', 'sub'), may hold values from 0.01 to 0.1
- group_kind: int32 [4], replicated, may hold values from 0 to 1, as said below
- partner: int32 [4], replicated, may hold values from 0 to 3, as said below
- surface_cell: int32 [4, 4096], P('grp', 'sub'), may hold values from 0 to 32767
- patch_count: int32 [4, 8], P('grp'), may hold values from 1 to 24, 64 in all within a row
- patch_centres: int32 [4, 192, 128], P('grp', 'sub'), may hold values from 0 to 4095, as said below
- patch_targets: int32 [4, 192, 128], P('grp', 'sub'), may hold values from 0 to 4095
- patch_maps: float32 [4, 192, 128, 128], P('grp', 'sub'), may hold values from -0.25 to 0.95
Outputs:
- temperature: float32 [4, 16, 16384], P('grp', 'sub')
- interface: float32 [4, 2, 4096], P('grp', None, 'sub')
Inputs may be any that keep to these rules, and one draw needn't show every extreme that they name: `group_kind`: both kinds occur. partner[g] is a group of the other kind than g. Slots 0 to patch_count[g, j] - 1 of device j of group g are live; each group's counts sum to 64; in each group some device holds 24. `patch_centres`: the centres of slot s of group g lie in the cyclic window of 1024 consecutive nodes that starts at (s // 24) * 512 - 512 // 2 + h[g], for one shift h[g] of each group.
All inputs are finite; a program needn't handle non-finite values.
Results may differ from a plain program's by a relative error of at most 0.00013.
Values sent between devices are 32-bit elements; how exact they have to be, the bound alone decides.
A program may use at most 64 MiB of HBM per device.

v0:
```python
import jax
import jax.numpy as jnp
from jax import lax
from jax.sharding import PartitionSpec as P

STEPS = 4
COUPLE = 4


def with_halo(cells, sides, width):
    for axis, dim in sides:
        count = lax.axis_size(axis)
        ends = count - 1
        head = lax.slice_in_dim(cells, 0, width, axis=dim)
        tail = lax.slice_in_dim(cells, cells.shape[dim] - width, cells.shape[dim], axis=dim)
        cells = jnp.concatenate(
            [
                lax.ppermute(tail, axis, [(i, (i + 1) % count) for i in range(ends)]),
                cells,
                lax.ppermute(head, axis, [((i + 1) % count, i) for i in range(ends)]),
            ],
            axis=dim,
        )
    return cells


def in_plane(current):
    return (
        jnp.roll(current, 1, -2)
        + jnp.roll(current, -1, -2)
        + jnp.roll(current, 1, -1)
        + jnp.roll(current, -1, -1)
    )


def advance(padded, conduct, velocity, heat_release, gas_mask):
    centre = padded[1:-1]
    upper_plane = padded[2:]
    lower_plane = padded[:-2]
    laplace = upper_plane + lower_plane + in_plane(centre) - 6.0 * centre
    return (
        centre
        + conduct * laplace
        - gas_mask * velocity * (centre - lower_plane)
        + gas_mask * heat_release * jax.nn.sigmoid(2.0 * centre)
    )


def local(
    initial_field,
    conduct,
    velocity,
    heat_release,
    group_kind,
    partner,
    surface_cell,
    patch_count,
    patch_centres,
    patch_targets,
    patch_maps,
):
    planes_here = initial_field.shape[1]
    plane_cells = initial_field.shape[2]
    slab_shape = (planes_here, plane_cells // 128, 128)
    current = initial_field.reshape(slab_shape)
    conduct_slab = conduct.reshape(slab_shape)
    velocity_slab = velocity.reshape(slab_shape)
    heat_slab = heat_release.reshape(slab_shape)
    sub_count = lax.axis_size("sub")
    slab_index = lax.axis_index("sub")
    group_index = lax.axis_index("grp")
    own_kind = group_kind[group_index]
    partner_row = partner[group_index]
    gas_mask = (own_kind == 0).astype(jnp.float32)
    gain_temp = jnp.where(own_kind == 0, 0.5, 0.25).astype(jnp.float32)
    gain_flux = jnp.where(own_kind == 0, -0.25, 0.25).astype(jnp.float32)
    surface = surface_cell[0]
    counts = patch_count[0]
    patch_mats = patch_maps[0]
    centres = patch_centres[0]
    targets = patch_targets[0]
    surf_here = surface.shape[0]
    node_total = surf_here * sub_count
    capacity = patch_mats.shape[0]
    live_mask = (jnp.arange(capacity, dtype=jnp.int32) < counts[slab_index]).astype(jnp.float32)
    interface = jnp.zeros((2, surf_here), jnp.float32)
    for iteration in range(COUPLE):
        for substep in range(STEPS):
            padded = with_halo(current, (("sub", 0),), 1)
            current = advance(padded, conduct_slab, velocity_slab, heat_slab, gas_mask)
        flux_field = conduct_slab * (4.0 * current - in_plane(current))
        flat_temp = current.reshape(-1)
        flat_flux = flux_field.reshape(-1)
        export = jnp.stack([flat_temp[surface], flat_flux[surface]])
        group_row = lax.all_gather(export, "sub", axis=1, tiled=True)
        every_row = lax.all_gather(group_row[None], "grp", axis=0, tiled=True)
        source = lax.dynamic_index_in_dim(every_row, partner_row, 0, keepdims=False)
        centre_vals = source[:, centres]
        contrib = (
            jnp.einsum("stk,qsk->qst", patch_mats, centre_vals, precision=lax.Precision.HIGHEST)
            * live_mask[None, :, None]
        )
        partial_rows = jnp.zeros((2, node_total), jnp.float32).at[:, targets].add(contrib)
        interface = lax.psum_scatter(partial_rows, "sub", scatter_dimension=1, tiled=True)
        increment = gain_temp * (interface[0] - export[0]) + gain_flux * interface[1]
        flat_temp = flat_temp.at[surface].add(increment)
        current = flat_temp.reshape(slab_shape)
    return (current.reshape(initial_field.shape), interface[None])


def solution(mesh):
    placed = (
        P("grp", "sub", None),
        P("grp", "sub", None),
        P("grp", "sub", None),
        P("grp", "sub", None),
        P(),
        P(),
        P("grp", "sub"),
        P("grp", None),
        P("grp", "sub", None),
        P("grp", "sub", None),
        P("grp", "sub", None, None),
    )
    return jax.shard_map(
        local,
        mesh=mesh,
        in_specs=placed,
        out_specs=(P("grp", "sub", None), P("grp", None, "sub")),
        check_vma=False,
    )
```

profile of v0, /device:TPU:0, one launch (start us, length us, event | category | flops | bytes accessed | tf_op | source)
XLA Modules:
  0.0 579.8 jit_solution(10298618127133347024)
XLA Ops:
  21.1 5.8 %collective-permute-start.3 = (f32[1,128,128]{2,1,0:T(8,128)S(1)}, f32[1,128,128]{2,1,0:T(8,128)S(1)}, u32[]{:S(2)}, u32[]{:S(2)}) collective-permute-start(f32[1,128,128]{2,1,0:T(8,128)S(1)} %get-tuple-element.197), channel_id=1, source_target_pairs={{0,1},{1,2},{2,3},{3,4},{4,5},{5,6},{6,7},{8,9},{9,10},{10,11},{11... | collective-permute-start | bytes 196616 | tf_op jit(solution)/shard_map/ppermute | solution.py:18
  29.5 4.7 collective-permute-start.5
  36.8 5.3 collective-permute-start.7
  43.4 3.1 gather_fusion
  46.7 3.1 gather_fusion.1
  49.9 17.8 %all_gather.24 = f32[2,4096]{1,0:T(2,128)S(1)} all-gather(f32[2,512]{1,0:T(2,128)S(1)} %pad_maximum_fusion.32), channel_id=1, replica_groups=mesh['grp'=4,'sub'=8] {'sub'}, dimensions={1}, use_global_device_ids=true | all-gather | bytes 36864 | tf_op jit(solution)/shard_map/all_gather | solution.py:95
  67.7 8.5 %all-gather.4 = f32[4,2,4096]{2,1,0:T(2,128)S(1)} all-gather(f32[1,2,4096]{2,1,0:T(2,128)S(1)} %bitcast.407), channel_id=2, replica_groups=mesh['grp'=4,'sub'=8] {'grp'}, dimensions={0}, use_global_device_ids=true | all-gather | bytes 163840 | tf_op jit(solution)/shard_map/all_gather | solution.py:96
  78.1 12.4 %gather_fusion.2 = f32[3072,2]{1,0:T(8,128)} fusion(f32[2,4096]{0,1:T(8,128)} %bitcast.398, s32[3072]{0:T(1024)S(1)} %fusion.206), kind=kCustom, calls=%fused_computation.2 | custom fusion | bytes 61440 | tf_op jit(solution)/shard_map/gather | solution.py:98
  92.4 2.6 fusion.11
  96.7 18.6 %scatter_custom_fusion = f32[2,4096]{0,1:T(8,128)} fusion(s32[3072]{0:T(1024)S(1)} %fusion.204, f32[3072,2]{1,0:T(8,128)} %copy.33, f32[]{:T(128)} %constant.47.clone.1), kind=kCustom, calls=%fused_computation.42 | custom fusion | flops 6144 | bytes 33280 | tf_op jit(solution)/shard_map/scatter-add | solution.py:103
  115.4 36.2 %reduce-scatter.5.cloned.1.call-done = f32[2,512]{0,1:T(8,128)} async-done(((f32[2,4096]{0,1:T(8,128)}), f32[2,512]{0,1:T(8,128)}) %reduce-scatter.5.cloned.1.call-update) | async-done | bytes 4112 | tf_op jit(solution)/shard_map/reduce_scatter | solution.py:104
  153.0 3.4 scatter_fusion
  157.9 3.0 collective-permute-start.9
  163.6 3.0 collective-permute-start.11
  169.2 5.4 collective-permute-start.13
  177.1 5.3 collective-permute-start.15
  183.7 3.1 gather_fusion.3
  187.0 3.1 gather_fusion.4
  190.1 16.6 %all_gather.26 = f32[2,4096]{1,0:T(2,128)S(1)} all-gather(f32[2,512]{1,0:T(2,128)S(1)} %pad_maximum_fusion.33), channel_id=1, replica_groups=mesh['grp'=4,'sub'=8] {'sub'}, dimensions={1}, use_global_device_ids=true | all-gather | bytes 36864 | tf_op jit(solution)/shard_map/all_gather | solution.py:95
  206.7 8.3 %all-gather.5 = f32[4,2,4096]{2,1,0:T(2,128)S(1)} all-gather(f32[1,2,4096]{2,1,0:T(2,128)S(1)} %bitcast.408), channel_id=3, replica_groups=mesh['grp'=4,'sub'=8] {'grp'}, dimensions={0}, use_global_device_ids=true | all-gather | bytes 163840 | tf_op jit(solution)/shard_map/all_gather | solution.py:96
  217.0 12.4 %gather_fusion.5 = f32[3072,2]{1,0:T(8,128)} fusion(f32[2,4096]{0,1:T(8,128)} %bitcast.399, s32[3072]{0:T(1024)S(1)} %fusion.206), kind=kCustom, calls=%fused_computation.5 | custom fusion | bytes 61440 | tf_op jit(solution)/shard_map/gather | solution.py:98
  235.6 18.6 %scatter_custom_fusion.2 = f32[2,4096]{0,1:T(8,128)} fusion(s32[3072]{0:T(1024)S(1)} %fusion.204, f32[3072,2]{1,0:T(8,128)} %copy.36, f32[]{:T(128)} %constant.47.clone.1), kind=kCustom, calls=%fused_computation.40 | custom fusion | flops 6144 | bytes 33280 | tf_op jit(solution)/shard_map/scatter-add | solution.py:103
  254.3 35.6 %reduce-scatter.7.cloned.1.call-done = f32[2,512]{0,1:T(8,128)} async-done(((f32[2,4096]{0,1:T(8,128)}), f32[2,512]{0,1:T(8,128)}) %reduce-scatter.7.cloned.1.call-update) | async-done | bytes 4112 | tf_op jit(solution)/shard_map/reduce_scatter | solution.py:104
  291.3 3.4 scatter_fusion.1
  296.2 3.0 collective-permute-start.17
  301.9 3.0 collective-permute-start.19
  307.5 5.3 collective-permute-start.21
  315.3 5.3 collective-permute-start.23
  322.0 3.1 gather_fusion.6
  325.3 3.1 gather_fusion.7
  328.4 16.8 %all_gather.28 = f32[2,4096]{1,0:T(2,128)S(1)} all-gather(f32[2,512]{1,0:T(2,128)S(1)} %pad_maximum_fusion.34), channel_id=1, replica_groups=mesh['grp'=4,'sub'=8] {'sub'}, dimensions={1}, use_global_device_ids=true | all-gather | bytes 36864 | tf_op jit(solution)/shard_map/all_gather | solution.py:95
  345.2 8.4 %all-gather.6 = f32[4,2,4096]{2,1,0:T(2,128)S(1)} all-gather(f32[1,2,4096]{2,1,0:T(2,128)S(1)} %bitcast.409), channel_id=4, replica_groups=mesh['grp'=4,'sub'=8] {'grp'}, dimensions={0}, use_global_device_ids=true | all-gather | bytes 163840 | tf_op jit(solution)/shard_map/all_gather | solution.py:96
  355.6 12.4 %gather_fusion.8 = f32[3072,2]{1,0:T(8,128)} fusion(f32[2,4096]{0,1:T(8,128)} %bitcast.400, s32[3072]{0:T(1024)S(1)} %fusion.206), kind=kCustom, calls=%fused_computation.8 | custom fusion | bytes 61440 | tf_op jit(solution)/shard_map/gather | solution.py:98
  374.2 18.6 %scatter_custom_fusion.4 = f32[2,4096]{0,1:T(8,128)} fusion(s32[3072]{0:T(1024)S(1)} %fusion.204, f32[3072,2]{1,0:T(8,128)} %copy.39, f32[]{:T(128)} %constant.47.clone.1), kind=kCustom, calls=%fused_computation.38 | custom fusion | flops 6144 | bytes 33280 | tf_op jit(solution)/shard_map/scatter-add | solution.py:103
  392.9 35.4 %reduce-scatter.9.cloned.1.call-done = f32[2,512]{0,1:T(8,128)} async-done(((f32[2,4096]{0,1:T(8,128)}), f32[2,512]{0,1:T(8,128)}) %reduce-scatter.9.cloned.1.call-update) | async-done | bytes 4112 | tf_op jit(solution)/shard_map/reduce_scatter | solution.py:104
  429.6 3.4 scatter_fusion.2
  434.5 3.0 collective-permute-start.25
  440.2 3.0 collective-permute-start.27
  445.8 5.3 collective-permute-start.29
  453.7 5.3 collective-permute-start.31
  460.3 3.1 gather_fusion.9
  463.6 3.1 gather_fusion.10
  466.7 16.6 %all_gather.30 = f32[2,4096]{1,0:T(2,128)S(1)} all-gather(f32[2,512]{1,0:T(2,128)S(1)} %pad_maximum_fusion.35), channel_id=1, replica_groups=mesh['grp'=4,'sub'=8] {'sub'}, dimensions={1}, use_global_device_ids=true | all-gather | bytes 36864 | tf_op jit(solution)/shard_map/all_gather | solution.py:95
  483.3 8.7 %all-gather.7 = f32[4,2,4096]{2,1,0:T(2,128)S(1)} all-gather(f32[1,2,4096]{2,1,0:T(2,128)S(1)} %bitcast.410), channel_id=5, replica_groups=mesh['grp'=4,'sub'=8] {'grp'}, dimensions={0}, use_global_device_ids=true | all-gather | bytes 163840 | tf_op jit(solution)/shard_map/all_gather | solution.py:96
  494.0 12.4 %gather_fusion.11 = f32[3072,2]{1,0:T(8,128)} fusion(f32[2,4096]{0,1:T(8,128)} %bitcast.397, s32[3072]{0:T(1024)S(1)} %fusion.206), kind=kCustom, calls=%fused_computation.11 | custom fusion | bytes 61440 | tf_op jit(solution)/shard_map/gather | solution.py:98
  512.6 18.6 %scatter_custom_fusion.6 = f32[2,4096]{0,1:T(8,128)} fusion(s32[3072]{0:T(1024)S(1)} %fusion.204, f32[3072,2]{1,0:T(8,128)} %copy.42, f32[]{:T(128)} %constant.47.clone.1), kind=kCustom, calls=%fused_computation.36 | custom fusion | flops 6144 | bytes 33280 | tf_op jit(solution)/shard_map/scatter-add | solution.py:103
  531.2 35.4 %reduce-scatter.11.cloned.1.call-done = f32[2,512]{0,1:T(8,128)} async-done(((f32[2,4096]{0,1:T(8,128)}), f32[2,512]{0,1:T(8,128)}) %reduce-scatter.11.cloned.1.call-update) | async-done | bytes 4112 | tf_op jit(solution)/shard_map/reduce_scatter | solution.py:104
  568.0 3.4 scatter_fusion.3
  (236 shorter events, 85.6 us)
Async XLA Ops:
  7.2 85.2 %copy-start = (f32[1,24,128,128]{3,2,1,0:T(8,128)S(1)}, f32[1,24,128,128]{3,2,1,0:T(8,128)}, u32[]{:S(2)}) copy-start(f32[1,24,128,128]{3,2,1,0:T(8,128)} %param.21) | copy-start | bytes 4718596
  7.2 8.8 %copy-start.8 = (s32[4]{0:T(128)S(1)}, s32[4]{0:T(128)}, u32[]{:S(2)}) copy-start(s32[4]{0:T(128)} %param.15) | copy-start | bytes 52
  7.2 10.1 %copy-start.7 = (s32[1,512]{1,0:T(1,128)S(1)}, s32[1,512]{1,0:T(1,128)}, u32[]{:S(2)}) copy-start(s32[1,512]{1,0:T(1,128)} %param.17) | copy-start | bytes 6148
  7.2 10.1 %copy-start.5 = (s32[1,24,128]{2,1,0:T(8,128)S(1)}, s32[1,24,128]{2,1,0:T(8,128)}, u32[]{:S(2)}) copy-start(s32[1,24,128]{2,1,0:T(8,128)} %param.19) | copy-start | bytes 36868
  7.2 10.1 %copy-start.6 = (s32[1,24,128]{2,1,0:T(8,128)S(1)}, s32[1,24,128]{2,1,0:T(8,128)}, u32[]{:S(2)}) copy-start(s32[1,24,128]{2,1,0:T(8,128)} %param.20) | copy-start | bytes 36868
  7.2 10.1 %copy-start.9 = (s32[1,8]{1,0:T(1,128)S(1)}, s32[1,8]{1,0:T(1,128)}, u32[]{:S(2)}) copy-start(s32[1,8]{1,0:T(1,128)} %param.18) | copy-start | bytes 100
  7.2 11.4 %copy-start.3 = (f32[1,2,16384]{2,1,0:T(2,128)S(1)}, f32[1,2,16384]{2,1,0:T(2,128)}, u32[]{:S(2)}) copy-start(f32[1,2,16384]{2,1,0:T(2,128)} %param.14) | copy-start | bytes 393220
  7.2 11.4 %copy-start.4 = (f32[1,2,16384]{2,1,0:T(2,128)S(1)}, f32[1,2,16384]{2,1,0:T(2,128)}, u32[]{:S(2)}) copy-start(f32[1,2,16384]{2,1,0:T(2,128)} %param.13) | copy-start | bytes 393220
  7.3 12.1 %copy-start.1 = (f32[1,2,16384]{2,1,0:T(2,128)S(1)}, f32[1,2,16384]{2,1,0:T(2,128)}, u32[]{:S(2)}) copy-start(f32[1,2,16384]{2,1,0:T(2,128)} %param.12) | copy-start | bytes 393220
  7.3 144.4 %reduce-scatter.5.cloned.1.call-start = ((), (), s32[]{:S(2)}) async-start(), calls=%async_computation.4 | async-start | bytes 2359296 | tf_op jit(solution)/shard_map/reduce_scatter | solution.py:104
  8.6 10.8 %collective-permute-start.1 = (f32[1,128,128]{2,1,0:T(8,128)S(1)}, f32[1,128,128]{2,1,0:T(8,128)S(1)}, u32[]{:S(2)}, u32[]{:S(2)}) collective-permute-start(f32[1,128,128]{2,1,0:T(8,128)S(1)} %bitcast.417), channel_id=1, source_target_pairs={{0,1},{1,2},{2,3},{3,4},{4,5},{5,6},{6,7},{8,9},{9,10},{10,11},{11... | collective-permute-start | bytes 196616 | tf_op jit(solution)/shard_map/ppermute | solution.py:18
  11.0 8.4 %collective-permute-start = (f32[1,128,128]{2,1,0:T(8,128)S(1)}, f32[1,128,128]{2,1,0:T(8,128)S(1)}, u32[]{:S(2)}, u32[]{:S(2)}) collective-permute-start(f32[1,128,128]{2,1,0:T(8,128)S(1)} %bitcast.416), channel_id=1, source_target_pairs={{1,0},{2,1},{3,2},{4,3},{5,4},{6,5},{7,6},{9,8},{10,9},{11,10},{12... | collective-permute-start | bytes 196616 | tf_op jit(solution)/shard_map/ppermute | solution.py:20
  19.8 7.2 %collective-permute-start.2 = (f32[1,128,128]{2,1,0:T(8,128)S(1)}, f32[1,128,128]{2,1,0:T(8,128)S(1)}, u32[]{:S(2)}, u32[]{:S(2)}) collective-permute-start(f32[1,128,128]{2,1,0:T(8,128)S(1)} %get-tuple-element.196), channel_id=1, source_target_pairs={{1,0},{2,1},{3,2},{4,3},{5,4},{6,5},{7,6},{9,8},{10,9},{11,10},{12... | collective-permute-start | bytes 196616 | tf_op jit(solution)/shard_map/ppermute | solution.py:20
  21.1 6.7 %collective-permute-start.3 = (f32[1,128,128]{2,1,0:T(8,128)S(1)}, f32[1,128,128]{2,1,0:T(8,128)S(1)}, u32[]{:S(2)}, u32[]{:S(2)}) collective-permute-start(f32[1,128,128]{2,1,0:T(8,128)S(1)} %get-tuple-element.197), channel_id=1, source_target_pairs={{0,1},{1,2},{2,3},{3,4},{4,5},{5,6},{6,7},{8,9},{9,10},{10,11},{11... | collective-permute-start | bytes 196616 | tf_op jit(solution)/shard_map/ppermute | solution.py:18
  28.2 6.0 %collective-permute-start.4 = (f32[1,128,128]{2,1,0:T(8,128)S(1)}, f32[1,128,128]{2,1,0:T(8,128)S(1)}, u32[]{:S(2)}, u32[]{:S(2)}) collective-permute-start(f32[1,128,128]{2,1,0:T(8,128)S(1)} %get-tuple-element.186), channel_id=1, source_target_pairs={{1,0},{2,1},{3,2},{4,3},{5,4},{6,5},{7,6},{9,8},{10,9},{11,10},{12... | collective-permute-start | bytes 196616 | tf_op jit(solution)/shard_map/ppermute | solution.py:20
  29.5 5.6 collective-permute-start.5
  35.5 6.6 %collective-permute-start.6 = (f32[1,128,128]{2,1,0:T(8,128)S(1)}, f32[1,128,128]{2,1,0:T(8,128)S(1)}, u32[]{:S(2)}, u32[]{:S(2)}) collective-permute-start(f32[1,128,128]{2,1,0:T(8,128)S(1)} %get-tuple-element.176), channel_id=1, source_target_pairs={{1,0},{2,1},{3,2},{4,3},{5,4},{6,5},{7,6},{9,8},{10,9},{11,10},{12... | collective-permute-start | bytes 196616 | tf_op jit(solution)/shard_map/ppermute | solution.py:20
  36.8 6.2 %collective-permute-start.7 = (f32[1,128,128]{2,1,0:T(8,128)S(1)}, f32[1,128,128]{2,1,0:T(8,128)S(1)}, u32[]{:S(2)}, u32[]{:S(2)}) collective-permute-start(f32[1,128,128]{2,1,0:T(8,128)S(1)} %get-tuple-element.177), channel_id=1, source_target_pairs={{0,1},{1,2},{2,3},{3,4},{4,5},{5,6},{6,7},{8,9},{9,10},{10,11},{11... | collective-permute-start | bytes 196616 | tf_op jit(solution)/shard_map/ppermute | solution.py:18
  115.3 174.6 %reduce-scatter.7.cloned.1.call-start = ((), (), s32[]{:S(2)}) async-start(), calls=%async_computation.5 | async-start | bytes 2359296 | tf_op jit(solution)/shard_map/reduce_scatter | solution.py:104
  156.6 4.4 collective-permute-start.8
  157.9 3.9 collective-permute-start.9
  162.3 4.4 collective-permute-start.10
  163.6 3.9 collective-permute-start.11
  167.9 6.8 %collective-permute-start.12 = (f32[1,128,128]{2,1,0:T(8,128)S(1)}, f32[1,128,128]{2,1,0:T(8,128)S(1)}, u32[]{:S(2)}, u32[]{:S(2)}) collective-permute-start(f32[1,128,128]{2,1,0:T(8,128)S(1)} %get-tuple-element.138), channel_id=1, source_target_pairs={{1,0},{2,1},{3,2},{4,3},{5,4},{6,5},{7,6},{9,8},{10,9},{11,10},{12... | collective-permute-start | bytes 196616 | tf_op jit(solution)/shard_map/ppermute | solution.py:20
  169.2 6.2 %collective-permute-start.13 = (f32[1,128,128]{2,1,0:T(8,128)S(1)}, f32[1,128,128]{2,1,0:T(8,128)S(1)}, u32[]{:S(2)}, u32[]{:S(2)}) collective-permute-start(f32[1,128,128]{2,1,0:T(8,128)S(1)} %get-tuple-element.139), channel_id=1, source_target_pairs={{0,1},{1,2},{2,3},{3,4},{4,5},{5,6},{6,7},{8,9},{9,10},{10,11},{11... | collective-permute-start | bytes 196616 | tf_op jit(solution)/shard_map/ppermute | solution.py:18
  175.8 6.6 %collective-permute-start.14 = (f32[1,128,128]{2,1,0:T(8,128)S(1)}, f32[1,128,128]{2,1,0:T(8,128)S(1)}, u32[]{:S(2)}, u32[]{:S(2)}) collective-permute-start(f32[1,128,128]{2,1,0:T(8,128)S(1)} %get-tuple-element.128), channel_id=1, source_target_pairs={{1,0},{2,1},{3,2},{4,3},{5,4},{6,5},{7,6},{9,8},{10,9},{11,10},{12... | collective-permute-start | bytes 196616 | tf_op jit(solution)/shard_map/ppermute | solution.py:20
  177.1 6.2 %collective-permute-start.15 = (f32[1,128,128]{2,1,0:T(8,128)S(1)}, f32[1,128,128]{2,1,0:T(8,128)S(1)}, u32[]{:S(2)}, u32[]{:S(2)}) collective-permute-start(f32[1,128,128]{2,1,0:T(8,128)S(1)} %get-tuple-element.129), channel_id=1, source_target_pairs={{0,1},{1,2},{2,3},{3,4},{4,5},{5,6},{6,7},{8,9},{9,10},{10,11},{11... | collective-permute-start | bytes 196616 | tf_op jit(solution)/shard_map/ppermute | solution.py:18
  254.3 174.0 %reduce-scatter.9.cloned.1.call-start = ((), (), s32[]{:S(2)}) async-start(), calls=%async_computation.6 | async-start | bytes 2359296 | tf_op jit(solution)/shard_map/reduce_scatter | solution.py:104
  294.9 4.4 collective-permute-start.16
  296.2 3.9 collective-permute-start.17
  300.6 4.4 collective-permute-start.18
  301.9 3.9 collective-permute-start.19
  306.2 6.6 %collective-permute-start.20 = (f32[1,128,128]{2,1,0:T(8,128)S(1)}, f32[1,128,128]{2,1,0:T(8,128)S(1)}, u32[]{:S(2)}, u32[]{:S(2)}) collective-permute-start(f32[1,128,128]{2,1,0:T(8,128)S(1)} %get-tuple-element.90), channel_id=1, source_target_pairs={{1,0},{2,1},{3,2},{4,3},{5,4},{6,5},{7,6},{9,8},{10,9},{11,10},{12... | collective-permute-start | bytes 196616 | tf_op jit(solution)/shard_map/ppermute | solution.py:20
  307.5 6.2 %collective-permute-start.21 = (f32[1,128,128]{2,1,0:T(8,128)S(1)}, f32[1,128,128]{2,1,0:T(8,128)S(1)}, u32[]{:S(2)}, u32[]{:S(2)}) collective-permute-start(f32[1,128,128]{2,1,0:T(8,128)S(1)} %get-tuple-element.91), channel_id=1, source_target_pairs={{0,1},{1,2},{2,3},{3,4},{4,5},{5,6},{6,7},{8,9},{9,10},{10,11},{11... | collective-permute-start | bytes 196616 | tf_op jit(solution)/shard_map/ppermute | solution.py:18
  314.0 6.6 %collective-permute-start.22 = (f32[1,128,128]{2,1,0:T(8,128)S(1)}, f32[1,128,128]{2,1,0:T(8,128)S(1)}, u32[]{:S(2)}, u32[]{:S(2)}) collective-permute-start(f32[1,128,128]{2,1,0:T(8,128)S(1)} %get-tuple-element.80), channel_id=1, source_target_pairs={{1,0},{2,1},{3,2},{4,3},{5,4},{6,5},{7,6},{9,8},{10,9},{11,10},{12... | collective-permute-start | bytes 196616 | tf_op jit(solution)/shard_map/ppermute | solution.py:20
  315.3 6.2 %collective-permute-start.23 = (f32[1,128,128]{2,1,0:T(8,128)S(1)}, f32[1,128,128]{2,1,0:T(8,128)S(1)}, u32[]{:S(2)}, u32[]{:S(2)}) collective-permute-start(f32[1,128,128]{2,1,0:T(8,128)S(1)} %get-tuple-element.81), channel_id=1, source_target_pairs={{0,1},{1,2},{2,3},{3,4},{4,5},{5,6},{6,7},{8,9},{9,10},{10,11},{11... | collective-permute-start | bytes 196616 | tf_op jit(solution)/shard_map/ppermute | solution.py:18
  392.8 173.8 %reduce-scatter.11.cloned.1.call-start = ((), (), s32[]{:S(2)}) async-start(), calls=%async_computation.7 | async-start | bytes 2359296 | tf_op jit(solution)/shard_map/reduce_scatter | solution.py:104
  433.2 4.4 collective-permute-start.24
  434.5 3.9 collective-permute-start.25
  438.9 4.4 collective-permute-start.26
  440.2 3.9 collective-permute-start.27
  444.5 6.6 %collective-permute-start.28 = (f32[1,128,128]{2,1,0:T(8,128)S(1)}, f32[1,128,128]{2,1,0:T(8,128)S(1)}, u32[]{:S(2)}, u32[]{:S(2)}) collective-permute-start(f32[1,128,128]{2,1,0:T(8,128)S(1)} %get-tuple-element.42), channel_id=1, source_target_pairs={{1,0},{2,1},{3,2},{4,3},{5,4},{6,5},{7,6},{9,8},{10,9},{11,10},{12... | collective-permute-start | bytes 196616 | tf_op jit(solution)/shard_map/ppermute | solution.py:20
  445.8 6.2 %collective-permute-start.29 = (f32[1,128,128]{2,1,0:T(8,128)S(1)}, f32[1,128,128]{2,1,0:T(8,128)S(1)}, u32[]{:S(2)}, u32[]{:S(2)}) collective-permute-start(f32[1,128,128]{2,1,0:T(8,128)S(1)} %get-tuple-element.43), channel_id=1, source_target_pairs={{0,1},{1,2},{2,3},{3,4},{4,5},{5,6},{6,7},{8,9},{9,10},{10,11},{11... | collective-permute-start | bytes 196616 | tf_op jit(solution)/shard_map/ppermute | solution.py:18
  452.4 6.6 %collective-permute-start.30 = (f32[1,128,128]{2,1,0:T(8,128)S(1)}, f32[1,128,128]{2,1,0:T(8,128)S(1)}, u32[]{:S(2)}, u32[]{:S(2)}) collective-permute-start(f32[1,128,128]{2,1,0:T(8,128)S(1)} %get-tuple-element.32), channel_id=1, source_target_pairs={{1,0},{2,1},{3,2},{4,3},{5,4},{6,5},{7,6},{9,8},{10,9},{11,10},{12... | collective-permute-start | bytes 196616 | tf_op jit(solution)/shard_map/ppermute | solution.py:20
  453.7 6.2 %collective-permute-start.31 = (f32[1,128,128]{2,1,0:T(8,128)S(1)}, f32[1,128,128]{2,1,0:T(8,128)S(1)}, u32[]{:S(2)}, u32[]{:S(2)}) collective-permute-start(f32[1,128,128]{2,1,0:T(8,128)S(1)} %get-tuple-element.33), channel_id=1, source_target_pairs={{0,1},{1,2},{2,3},{3,4},{4,5},{5,6},{6,7},{8,9},{9,10},{10,11},{11... | collective-permute-start | bytes 196616 | tf_op jit(solution)/shard_map/ppermute | solution.py:18
  567.9 4.2 copy-start.2
Sparse Core Ops, SparseCore 0:
  115.4 36.1 reduce-scatter.4
  254.4 35.4 reduce-scatter.6
  392.9 35.2 reduce-scatter.8
  531.3 35.2 reduce-scatter.10
where the time goes:
time: 589 us; the launch traced here: 580 us
  waiting for transfers between devices  155 us (26%)
  local copies, waits for them, and re-layouts  108 us (18%)
  blocking collectives  102 us (17%)
  other arithmetic  97.4 us (17%)
  starting transfers between devices  89.3 us (15%)
  between operations  18.4 us (3%)
  matrix products  10.2 us (2%)
    reduce_scatter x4, waiting for transfers between devices, local(): lax.psum_scatter(partial_rows, 'sub', scatter_dimension=1, tiled=True)  143 us
    scatter-add x4, other arithmetic, local(): jnp.zeros((2, node_total), jnp.float32).at[:, targets].add(contrib)  74.5 us
    ppermute x16, starting transfers between devices, with_halo(): lax.ppermute(tail, axis, [(i, (i + 1) % count) for i in range(ends)])  68.4 us
    all_gather x4, blocking collectives, local(): group_row = lax.all_gather(export, 'sub', axis=1, tiled=True)  67.8 us
    gather x8, local copies, waits for them, and re-layouts, local(): centre_vals = source[:, centres]  57.2 us
    all_gather x4, blocking collectives, local(): every_row = lax.all_gather(group_row[None], 'grp', axis=0, tiled=True)  33.9 us
    gather x8, local copies, waits for them, and re-layouts, local(): export = jnp.stack([flat_temp[surface], flat_flux[surface]])  25.1 us
    ppermute x16, starting transfers between devices, with_halo(): lax.ppermute(head, axis, [((i + 1) % count, i) for i in range(ends)])  20.7 us
  transfers between devices with their start and end apart: 36, of which 19 were waited for; matrix products, arithmetic and copies ran while one was open for 1% of the time, Pallas kernels for 0%

commit v1 on v0

v1 whole, which is shorter than its diff:
```python
import jax
import jax.numpy as jnp
from jax import lax
from jax.experimental import pallas as pl
from jax.experimental.pallas import tpu as pltpu
from jax.sharding import PartitionSpec as P

STEPS = 4
COUPLE = 4
LANES = 128
F32 = jnp.float32
BF16 = jnp.bfloat16


def split(x):
    hi = x.astype(BF16).astype(F32)
    return hi, x - hi


def dot_nt(a, b):
    return lax.dot_general(a, b, (((1,), (1,)), ((), ())), preferred_element_type=F32)


def dot_nn(a, b):
    return lax.dot_general(a, b, (((1,), (0,)), ((), ())), preferred_element_type=F32)


def iota(shape, dim):
    return lax.broadcasted_iota(jnp.int32, shape, dim)


def in_plane(c):
    rows, cols = c.shape
    return (
        pltpu.roll(c, 1, 0)
        + pltpu.roll(c, rows - 1, 0)
        + pltpu.roll(c, 1, 1)
        + pltpu.roll(c, cols - 1, 1)
    )


def kernel(
    n,
    groups,
    kind_ref,
    partner_ref,
    count_ref,
    field_ref,
    cond_ref,
    vel_ref,
    heat_ref,
    surf_ref,
    cent_ref,
    targ_ref,
    maps_ref,
    out_ref,
    iface_ref,
    fa,
    fb,
    cx,
    vx,
    hx,
    land,
    surf_all,
    oh_surf,
    oh_cent,
    oh_targ,
    maps2,
    exp_buf,
    grp_land,
    sel_buf,
    gath,
    part,
    rs_land,
    inc_buf,
    inc_land,
    set_send,
    set_recv,
    grp_send,
    grp_recv,
    ga_send,
    ga_recv,
    rs_send,
    rs_recv,
    inc_send,
    inc_recv,
    halo_send,
    halo_recv,
):
    planes, rows, cols = field_ref.shape
    surf_here = surf_ref.shape[1]
    cap = cent_ref.shape[0]
    reach = -(-STEPS // planes)
    depth = reach * planes
    ext = planes + 2 * depth
    offs = [d for d in range(-reach, reach + 1) if d != 0]
    at = {d: i for i, d in enumerate(offs)}
    tile = 2 * surf_here // LANES
    half = surf_here // LANES
    me = lax.axis_index("sub")
    grp = lax.axis_index("grp")

    def there(d):
        return jnp.logical_and(me + d >= 0, me + d < n)

    def rcopy(src, dst, ss, rs, dev):
        return pltpu.make_async_remote_copy(
            src_ref=src,
            dst_ref=dst,
            send_sem=ss,
            recv_sem=rs,
            device_id=dev,
            device_id_type=pl.DeviceIdType.MESH,
        )

    for buf in (fa, cx, vx, hx):
        buf[...] = jnp.zeros(buf.shape, F32)
    land[...] = jnp.zeros(land.shape, F32)
    inc_land[...] = jnp.zeros(inc_land.shape, F32)
    surf_all[...] = jnp.zeros(surf_all.shape, jnp.int32)

    barrier = pltpu.get_barrier_semaphore()
    for k in range(1, n):
        pl.semaphore_signal(
            barrier, inc=1, device_id={"sub": lax.rem(me + k, n)}, device_id_type=pl.DeviceIdType.MESH
        )
    for k in range(1, groups):
        pl.semaphore_signal(
            barrier, inc=1, device_id={"grp": lax.rem(grp + k, groups)}, device_id_type=pl.DeviceIdType.MESH
        )
    pl.semaphore_wait(barrier, n - 1 + groups - 1)

    def coef_span(slot_d):
        base = depth + planes * slot_d
        return base, max(1, base) - base, min(ext - 1, base + planes) - base

    def setup_copies(to, slot):
        base, lo, hi = coef_span(slot)
        dev = {"sub": me + to}
        ss, rs = at[to], at[slot]
        pairs = [(field_ref, fa.at[pl.ds(base, planes)])]
        for src, dst in ((cond_ref, cx), (vel_ref, vx), (heat_ref, hx)):
            pairs.append((src.at[pl.ds(lo, hi - lo)], dst.at[pl.ds(base + lo, hi - lo)]))
        pairs.append((surf_ref, surf_all.at[slot + reach]))
        return [
            rcopy(s, t, set_send.at[j, ss], set_recv.at[j, rs], dev) for j, (s, t) in enumerate(pairs)
        ]

    for d in sorted(offs, key=abs):

        @pl.when(there(d))
        def _():
            for c in setup_copies(d, -d):
                c.start()

    kind = kind_ref[grp]
    gas = jnp.where(kind == 0, 1.0, 0.0).astype(F32)
    gain_t = jnp.where(kind == 0, 0.5, 0.25).astype(F32)
    gain_f = jnp.where(kind == 0, -0.25, 0.25).astype(F32)
    partner = partner_ref[grp]
    count = count_ref[0, me]
    own = pl.ds(depth, planes)
    fa[own] = field_ref[...]
    cx[own] = cond_ref[...]
    vx[own] = vel_ref[...]
    hx[own] = heat_ref[...]
    surf_all[reach] = surf_ref[...]
    node_row = iota((n * tile, LANES), 0)
    node_row = (node_row // tile) * half + node_row % half
    for s in range(cap):
        lanes = pl.ds(s * LANES, LANES)
        hit = (node_row == cent_ref[s : s + 1, :] // LANES).astype(F32).astype(BF16)
        oh_cent[pl.ds(0, n * tile), lanes] = hit
        oh_cent[pl.ds(n * tile, n * tile), lanes] = hit
        oh_targ[:, lanes] = (node_row == targ_ref[s : s + 1, :] // LANES).astype(F32).astype(BF16)
        live = jnp.where(s < count, 1.0, 0.0).astype(F32)
        hi, lo = split(maps_ref[s] * live)
        maps2[s, pl.ds(0, LANES)] = hi.astype(BF16)
        maps2[s, pl.ds(LANES, LANES)] = lo.astype(BF16)

    for d in offs:

        @pl.when(there(d))
        def _():
            for c in setup_copies(-d, d):
                c.wait_recv()
            for c in setup_copies(d, -d):
                c.wait_send()

    vx[...] = vx[...] * gas
    hx[...] = hx[...] * gas
    cell_row = iota((planes * rows, surf_here), 0)
    for j in range(2 * reach + 1):
        oh_surf[j] = (cell_row == surf_all[j] // LANES).astype(F32).astype(BF16)

    lane_of = iota((LANES, surf_here), 0)
    group_of_slots = 4 if cap % 4 == 0 else 1
    width = group_of_slots * LANES
    lane_of_chunk = iota((LANES, width), 0)
    q_of_row = iota((n * tile, LANES), 0) % tile >= half

    def step(src, dst, k):
        for z in range(k + 1, ext - k - 1):
            c = src[z]
            dn = src[z - 1]
            lap = src[z + 1] + dn + in_plane(c) - 6.0 * c
            dst[z] = c + cx[z] * lap - vx[z] * (c - dn) + hx[z] * jax.nn.sigmoid(2.0 * c)

    def as_row(t8):
        return jnp.concatenate([t8[i : i + 1, :] for i in range(half)], axis=1)

    def spread(slot, t8):
        hi, lo = split(as_row(t8))
        mine = lane_of == surf_all[slot] % LANES
        rhs = jnp.concatenate(
            [jnp.where(mine, hi, 0.0).astype(BF16), jnp.where(mine, lo, 0.0).astype(BF16)], axis=0
        )
        r = dot_nt(oh_surf[slot], rhs)
        return (r[:, :LANES] + r[:, LANES:]).reshape(planes, rows, LANES)

    def halo_copy(par, to, slot):
        return rcopy(
            fa.at[own],
            land.at[par, at[slot]],
            halo_send.at[par, at[to]],
            halo_recv.at[par, at[slot]],
            {"sub": me + to},
        )

    def inc_copy(to, slot):
        return rcopy(
            inc_buf, inc_land.at[at[slot]], inc_send.at[at[to]], inc_recv.at[at[slot]], {"sub": me + to}
        )

    def grp_copy(par, k):
        return rcopy(
            exp_buf,
            grp_land.at[par, k - 1],
            grp_send.at[par, k - 1],
            grp_recv.at[par, k - 1],
            {"grp": lax.rem(grp + k, groups)},
        )

    def gath_copy(k, sender):
        return rcopy(sel_buf, gath.at[sender], ga_send.at[k - 1], ga_recv.at[k - 1], {"sub": lax.rem(me + k, n)})

    def rs_copy(k, sender):
        peer = lax.rem(me + k, n)
        return rcopy(part.at[peer], rs_land.at[sender], rs_send.at[k - 1], rs_recv.at[k - 1], {"sub": peer})

    def couple(it, carry):
        par = lax.rem(it, 2)
        last = it == COUPLE - 1
        pair = (fa, fb)
        for k in range(STEPS):
            step(pair[k % 2], pair[(k + 1) % 2], k)
        final = pair[STEPS % 2]

        temp = jnp.concatenate([final[depth + p].T for p in range(planes)], axis=1)
        flux = jnp.concatenate(
            [
                (cx[depth + p] * (4.0 * final[depth + p] - in_plane(final[depth + p]))).T
                for p in range(planes)
            ],
            axis=1,
        )
        pieces = [x.astype(BF16) for v in (temp, flux) for x in split(v)]
        got = dot_nn(jnp.concatenate(pieces, axis=0), oh_surf[reach])
        mine = lane_of == surf_all[reach] % LANES
        for q in range(2):
            v = got[2 * q * LANES : (2 * q + 1) * LANES] + got[(2 * q + 1) * LANES : (2 * q + 2) * LANES]
            v = jnp.sum(jnp.where(mine, v, 0.0), axis=0, keepdims=True)
            for i in range(half):
                exp_buf[q * half + i : q * half + i + 1, :] = v[:, i * LANES : (i + 1) * LANES]

        for k in range(1, groups):
            grp_copy(par, k).start()
        for k in range(1, groups):
            grp_copy(par, k).wait_recv()
        sel = jnp.zeros((tile, LANES), F32)
        for k in range(1, groups):
            source = lax.rem(grp + groups - k, groups)
            sel = jnp.where(partner == source, grp_land[par, k - 1], sel)
        sel_buf[...] = sel
        for k in range(1, n):
            gath_copy(k, me).start()
        gath[me] = sel

        for d in offs:

            @pl.when(jnp.logical_and(there(d), jnp.logical_not(last)))
            def _():
                halo_copy(par, d, -d).start()

        for k in range(1, n):
            gath_copy(k, lax.rem(me + n - k, n)).wait_recv()

        src = gath[...].reshape(n * tile, LANES)
        both = jnp.concatenate([jnp.where(q_of_row, 0.0, src), jnp.where(q_of_row, src, 0.0)], axis=1)
        hi, lo = split(both)
        lhs = jnp.concatenate([hi, lo], axis=0).T.astype(BF16)
        acc = jnp.zeros((n * tile, 4 * LANES), F32)
        for s0 in range(0, cap, group_of_slots):
            lanes = slice(s0 * LANES, s0 * LANES + width)
            slots = range(s0, s0 + group_of_slots)
            cent = jnp.concatenate([cent_ref[s : s + 1, :] for s in slots], axis=1) % LANES
            vals = dot_nn(lhs, oh_cent[:, lanes])
            hit = lane_of_chunk == cent
            cv = [
                jnp.sum(jnp.where(hit, vals[q * LANES : (q + 1) * LANES], 0.0), axis=0, keepdims=True)
                for q in range(2)
            ]
            hi, lo = split(jnp.concatenate(cv, axis=0))
            c4 = jnp.concatenate([hi, lo], axis=0).astype(BF16)
            contrib = []
            for i, s in enumerate(slots):
                r = dot_nt(c4[:, i * LANES : (i + 1) * LANES], maps2[s])
                r = r[:, :LANES] + r[:, LANES:]
                contrib.append(r[0:2] + r[2:4])
            hi, lo = split(jnp.concatenate(contrib, axis=1))
            targ = jnp.concatenate([targ_ref[s : s + 1, :] for s in slots], axis=1) % LANES
            hit = lane_of_chunk == targ
            rhs = jnp.concatenate(
                [jnp.where(hit, x[q : q + 1], 0.0).astype(BF16) for q in range(2) for x in (hi, lo)], axis=0
            )
            acc = acc + dot_nt(oh_targ[:, lanes], rhs)
        p0 = acc[:, :LANES] + acc[:, LANES : 2 * LANES]
        p1 = acc[:, 2 * LANES : 3 * LANES] + acc[:, 3 * LANES :]
        part[...] = jnp.where(q_of_row, p1, p0).reshape(n, tile, LANES)
        for k in range(1, n):
            rs_copy(k, me).start()
        rs_land[me] = part[me]
        for k in range(1, n):
            rs_copy(k, lax.rem(me + n - k, n)).wait_recv()
        iface = rs_land[0]
        for j in range(1, n):
            iface = iface + rs_land[j]
        iface_ref[...] = iface
        inc = gain_t * (iface - exp_buf[...]) + pltpu.roll(gain_f * iface, half, 0)
        inc_buf[...] = inc
        for d in offs:

            @pl.when(jnp.logical_and(there(d), jnp.logical_not(last)))
            def _():
                inc_copy(d, -d).start()
                halo_copy(par, d, -d).wait_send()

        fa[own] = final[own] + spread(reach, inc)

        @pl.when(jnp.logical_not(last))
        def _():
            for d in offs:

                @pl.when(there(d))
                def _():
                    halo_copy(par, -d, d).wait_recv()
                    inc_copy(-d, d).wait_recv()

                fa[pl.ds(depth + planes * d, planes)] = land[par, at[d]] + spread(d + reach, inc_land[at[d]])
            for d in offs:

                @pl.when(there(d))
                def _():
                    inc_copy(d, -d).wait_send()

        for k in range(1, groups):
            grp_copy(par, k).wait_send()
        for k in range(1, n):
            gath_copy(k, me).wait_send()
            rs_copy(k, me).wait_send()
        return carry

    lax.fori_loop(0, COUPLE, couple, 0)
    out_ref[...] = fa[own]


def local_of(n, groups):
    def local(
        initial_field,
        conduct,
        velocity,
        heat_release,
        group_kind,
        partner,
        surface_cell,
        patch_count,
        patch_centres,
        patch_targets,
        patch_maps,
    ):
        _, planes, cells = initial_field.shape
        rows = cells // LANES
        slab = (planes, rows, LANES)
        surf_here = surface_cell.shape[1]
        cap = patch_centres.shape[1]
        reach = -(-STEPS // planes)
        ext = planes + 2 * reach * planes
        tile = 2 * surf_here // LANES
        vmem = pl.BlockSpec(memory_space=pltpu.VMEM)
        smem = pl.BlockSpec(memory_space=pltpu.SMEM)
        dma = pltpu.SemaphoreType.DMA
        nd = 2 * reach
        scratch = [
            pltpu.VMEM((ext, rows, LANES), F32),
            pltpu.VMEM((ext, rows, LANES), F32),
            pltpu.VMEM((ext, rows, LANES), F32),
            pltpu.VMEM((ext, rows, LANES), F32),
            pltpu.VMEM((ext, rows, LANES), F32),
            pltpu.VMEM((2, nd, planes, rows, LANES), F32),
            pltpu.VMEM((nd + 1, 1, surf_here), jnp.int32),
            pltpu.VMEM((nd + 1, planes * rows, surf_here), BF16),
            pltpu.VMEM((2 * n * tile, cap * LANES), BF16),
            pltpu.VMEM((n * tile, cap * LANES), BF16),
            pltpu.VMEM((cap, 2 * LANES, LANES), BF16),
            pltpu.VMEM((tile, LANES), F32),
            pltpu.VMEM((2, groups - 1, tile, LANES), F32),
            pltpu.VMEM((tile, LANES), F32),
            pltpu.VMEM((n, tile, LANES), F32),
            pltpu.VMEM((n, tile, LANES), F32),
            pltpu.VMEM((n, tile, LANES), F32),
            pltpu.VMEM((tile, LANES), F32),
            pltpu.VMEM((nd, tile, LANES), F32),
            dma((5, nd)),
            dma((5, nd)),
            dma((2, groups - 1)),
            dma((2, groups - 1)),
            dma((n - 1,)),
            dma((n - 1,)),
            dma((n - 1,)),
            dma((n - 1,)),
            dma((nd,)),
            dma((nd,)),
            dma((2, nd)),
            dma((2, nd)),
        ]

        def body(*refs):
            kernel(n, groups, *refs)

        field, iface = pl.pallas_call(
            body,
            name="coupled",
            out_shape=(
                jax.ShapeDtypeStruct(slab, F32),
                jax.ShapeDtypeStruct((tile, LANES), F32),
            ),
            in_specs=[smem] * 3 + [vmem] * 8,
            out_specs=(vmem, vmem),
            scratch_shapes=scratch,
            compiler_params=pltpu.CompilerParams(
                collective_id=0, has_side_effects=True, vmem_limit_bytes=56 * 1024 * 1024
            ),
        )(
            group_kind,
            partner,
            patch_count,
            initial_field.reshape(slab),
            conduct.reshape(slab),
            velocity.reshape(slab),
            heat_release.reshape(slab),
            surface_cell,
            patch_centres[0],
            patch_targets[0],
            patch_maps[0],
        )
        return field.reshape(initial_field.shape), iface.reshape(1, 2, surf_here)

    return local


def solution(mesh):
    placed = (
        P("grp", "sub", None),
        P("grp", "sub", None),
        P("grp", "sub", None),
        P("grp", "sub", None),
        P(),
        P(),
        P("grp", "sub"),
        P("grp", None),
        P("grp", "sub", None),
        P("grp", "sub", None),
        P("grp", "sub", None, None),
    )
    return jax.shard_map(
        local_of(mesh.shape["sub"], mesh.shape["grp"]),
        mesh=mesh,
        in_specs=placed,
        out_specs=(P("grp", "sub", None), P("grp", None, "sub")),
        check_vma=False,
    )
```

time: 589 us -> 101 us (0.17); the launches traced: 580 us -> 101 us
  waiting for transfers between devices: 155 us -> 0 us
  blocking collectives: 102 us -> 0 us
  local copies, waits for them, and re-layouts: 108 us -> 6.28 us
  other arithmetic: 97.4 us -> 0 us
  Pallas kernels: 0 us -> 93.9 us
  starting transfers between devices: 89.3 us -> 0 us
  between operations: 18.4 us -> 0.64 us
  matrix products: 10.2 us -> 0 us
    reduce_scatter x4 -> x0, waiting for transfers between devices: 143 us -> none  [local(): lax.psum_scatter(partial_rows, 'sub', scatter_dimension=1, tiled=True)]
    all_gather x8 -> x0, blocking collectives: 102 us -> none  [the longest x4 67.8 us: local(): group_row = lax.all_gather(export, 'sub', axis=1, tiled=True)]
    pallas_call x0 -> x1, Pallas kernels: none -> 93.9 us  [local(): pl.pallas_call(body, name='coupled', out_shape=(jax.ShapeDtypeStruct(slab...]
    ppermute x32 -> x0, starting transfers between devices: 89.1 us -> none  [the longest x16 68.4 us: with_halo(): lax.ppermute(tail, axis, [(i, (i + 1) % count) for i in range(ends)])]
    scatter-add x8 -> x0, other arithmetic: 88.2 us -> none  [the longest x4 74.5 us: local(): jnp.zeros((2, node_total), jnp.float32).at[:, targets].add(contrib)]
    gather x16 -> x0, local copies, waits for them, and re-layouts: 82.3 us -> none  [the longest x8 57.2 us: local(): centre_vals = source[:, centres]]
    ppermute x32 -> x0, waiting for transfers between devices: 12.7 us -> none  [the longest x16 12.7 us: with_halo(): lax.ppermute(tail, axis, [(i, (i + 1) % count) for i in range(ends)])]
    dynamic_slice x11 -> x0, local copies, waits for them, and re-layouts: 10.3 us -> none  [the longest x8 7.88 us: local(): source = lax.dynamic_index_in_dim(every_row, partner_row, 0, keepdims=False)]
  transfers between devices with their start and end apart: 36 -> 0, of which waited for: 19 -> 0; matrix products, arithmetic and copies ran while one was open for 1% -> 0% of each run, Pallas kernels for 0% -> 0%
where the time goes in v1:
time: 101 us
  Pallas kernels  93.9 us (93%)
  local copies, waits for them, and re-layouts  6.28 us (6%)
    pallas_call x1, Pallas kernels, local(): pl.pallas_call(body, name='coupled', out_shape=(jax.ShapeDtypeStruct(slab...  93.9 us
    reshape x2, local copies, waits for them, and re-layouts, local(): return (field.reshape(initial_field.shape), iface.reshape(1, 2, surf_here))  2.91 us

profile of v1, /device:TPU:0, one launch (start us, length us, event | category | flops | bytes accessed | tf_op | source)
XLA Modules:
  0.0 100.9 jit_solution(12427745329135527806)
XLA Ops:
  0.6 1.7 %copy_bitcast_fusion.2 = (f32[2,128,128]{2,1,0:T(8,128)}, f32[2,128,128]{2,1,0:T(8,128)}) fusion(f32[1,2,128,128]{3,1,2,0:T(2,128)} %bitcast.20, f32[1,2,128,128]{3,1,2,0:T(2,128)} %bitcast.21), kind=kLoop, calls=%fused_computation.2 | loop fusion | bytes 524288 | tf_op jit(solution)/shard_map/reshape | solution.py:458
  2.3 1.7 %copy_bitcast_fusion = (f32[2,128,128]{2,1,0:T(8,128)}, f32[2,128,128]{2,1,0:T(8,128)}) fusion(f32[1,2,128,128]{3,1,2,0:T(2,128)} %bitcast.22, f32[1,2,128,128]{3,1,2,0:T(2,128)} %bitcast.23), kind=kLoop, calls=%fused_computation | loop fusion | bytes 524288 | tf_op jit(solution)/shard_map/reshape | solution.py:460
  4.0 93.9 %coupled.1 = (f32[2,128,128]{2,1,0:T(8,128)}, f32[8,128]{1,0:T(8,128)}) custom-call(s32[4]{0:T(128)} %refs_0_.1, s32[4]{0:T(128)} %refs_1_.1, s32[1,8]{1,0:T(1,128)} %refs_2_.1, f32[2,128,128]{2,1,0:T(8,128)} %get-tuple-element.9.refs_3_, f32[2,128,128]{2,1,0:T(8,128)} %get-tuple-element.8.refs_4_, f32[2,128,128]{2,1,0:T(8,128)} %get-tuple-element.7.refs_5_, ...), custom_call_target="tpu_custom_call" | custom-call | tf_op jit(solution)/shard_map/coupled/pallas_call | solution.py:440
  97.9 1.6 %reshape.26 = f32[1,2,16384]{2,1,0:T(2,128)} reshape(f32[2,128,128]{2,1,0:T(8,128)} %get-tuple-element.4) | data formatting | bytes 262144 | tf_op jit(solution)/shard_map/reshape | solution.py:466
  99.6 1.3 %reshape.27 = f32[1,2,512]{2,1,0:T(2,128)} reshape(f32[8,128]{1,0:T(8,128)} %get-tuple-element.5) | data formatting | bytes 8192 | tf_op jit(solution)/shard_map/reshape | solution.py:466

commit v2 on v1

--- a/solution.py
+++ b/solution.py
@@ -86,8 +86,13 @@
     inc_recv,
     halo_send,
     halo_recv,
+    maps,
+    load_sem,
 ):
-    planes, rows, cols = field_ref.shape
+    planes = field_ref.shape[1]
+    rows = fa.shape[1]
+    near = STEPS // 2
+    assert near % 2 == 0 and near <= planes
     surf_here = surf_ref.shape[1]
     cap = cent_ref.shape[0]
     reach = -(-STEPS // planes)
@@ -113,6 +118,9 @@
             device_id_type=pl.DeviceIdType.MESH,
         )
 
+    load = pltpu.make_async_copy(maps_ref, maps, load_sem)
+    load.start()
+
     for buf in (fa, cx, vx, hx):
         buf[...] = jnp.zeros(buf.shape, F32)
     land[...] = jnp.zeros(land.shape, F32)
@@ -128,30 +136,95 @@
         pl.semaphore_signal(
             barrier, inc=1, device_id={"grp": lax.rem(grp + k, groups)}, device_id_type=pl.DeviceIdType.MESH
         )
+
+    own = pl.ds(depth, planes)
+    fetch = ((field_ref, fa), (cond_ref, cx), (vel_ref, vx), (heat_ref, hx))
+
+    def unfold(b, carry):
+        chunk = pl.ds(pl.multiple_of(b * 8 * LANES, LANES), 8 * LANES)
+        for src, dst in fetch:
+            x = src[0, :, chunk]
+            for p in range(planes):
+                dst[depth + p, pl.ds(pl.multiple_of(b * 8, 8), 8), :] = jnp.concatenate(
+                    [x[p : p + 1, i * LANES : (i + 1) * LANES] for i in range(8)], axis=0
+                )
+        return carry
+
+    lax.fori_loop(0, rows // 8, unfold, 0)
     pl.semaphore_wait(barrier, n - 1 + groups - 1)
 
-    def coef_span(slot_d):
-        base = depth + planes * slot_d
-        return base, max(1, base) - base, min(ext - 1, base + planes) - base
-
-    def setup_copies(to, slot):
-        base, lo, hi = coef_span(slot)
-        dev = {"sub": me + to}
-        ss, rs = at[to], at[slot]
-        pairs = [(field_ref, fa.at[pl.ds(base, planes)])]
-        for src, dst in ((cond_ref, cx), (vel_ref, vx), (heat_ref, hx)):
-            pairs.append((src.at[pl.ds(lo, hi - lo)], dst.at[pl.ds(base + lo, hi - lo)]))
-        pairs.append((surf_ref, surf_all.at[slot + reach]))
+    def send_planes(buf, lo, hi, to, j):
+        slot = -to
+        shift = depth - (depth + planes * slot)
+        return rcopy(
+            buf.at[pl.ds(lo + shift, hi - lo)],
+            buf.at[pl.ds(lo, hi - lo)],
+            set_send.at[j, at[to]],
+            set_recv.at[j, at[slot]],
+            {"sub": me + to},
+        )
+
+    def first_copies(to):
+        base = depth - planes * to
+        lo, hi = max(base, depth - near), min(base + planes, depth + planes + near)
+        out = [send_planes(fa, lo, hi, to, 0)]
+        lo, hi = max(base, depth - near + 1), min(base + planes, depth + planes + near - 1)
+        if hi > lo:
+            out += [send_planes(buf, lo, hi, to, j + 1) for j, buf in enumerate((cx, vx, hx))]
+        return out
+
+    def rest_copies(to, which):
+        base = depth - planes * to
+        lo, hi = max(base, 1), min(base + planes, ext - 1)
+        if to == 1:
+            hi = min(hi, depth - near + 1)
+        if to == -1:
+            lo = max(lo, depth + planes + near - 1)
+        if hi <= lo:
+            return []
+        return [send_planes((cx, vx, hx)[j], lo, hi, to, j + 4) for j in which]
+
+    def surf_copies(to):
         return [
-            rcopy(s, t, set_send.at[j, ss], set_recv.at[j, rs], dev) for j, (s, t) in enumerate(pairs)
+            rcopy(
+                surf_ref,
+                surf_all.at[reach - to],
+                set_send.at[7, at[to]],
+                set_recv.at[7, at[-to]],
+                {"sub": me + to},
+            )
         ]
 
-    for d in sorted(offs, key=abs):
-
-        @pl.when(there(d))
-        def _():
-            for c in setup_copies(d, -d):
-                c.start()
+    def mid_copy(to):
+        return rcopy(
+            fa.at[own],
+            land.at[1, at[-to]],
+            set_send.at[8, at[to]],
+            set_recv.at[8, at[-to]],
+            {"sub": me + to},
+        )
+
+    def each(ds, act):
+        for d in ds:
+
+            @pl.when(there(d))
+            def _():
+                act(d)
+
+    def starts(copies):
+        for c in copies:
+            c.start()
+
+    def arrivals(copies):
+        for c in copies:
+            c.wait_recv()
+
+    def departures(copies):
+        for c in copies:
+            c.wait_send()
+
+    beside = (-1, 1)
+    each(beside, lambda d: starts(first_copies(d)))
 
     kind = kind_ref[grp]
     gas = jnp.where(kind == 0, 1.0, 0.0).astype(F32)
@@ -159,14 +232,10 @@
     gain_f = jnp.where(kind == 0, -0.25, 0.25).astype(F32)
     partner = partner_ref[grp]
     count = count_ref[0, me]
-    own = pl.ds(depth, planes)
-    fa[own] = field_ref[...]
-    cx[own] = cond_ref[...]
-    vx[own] = vel_ref[...]
-    hx[own] = heat_ref[...]
     surf_all[reach] = surf_ref[...]
     node_row = iota((n * tile, LANES), 0)
     node_row = (node_row // tile) * half + node_row % half
+    load.wait()
     for s in range(cap):
         lanes = pl.ds(s * LANES, LANES)
         hit = (node_row == cent_ref[s : s + 1, :] // LANES).astype(F32).astype(BF16)
@@ -174,24 +243,16 @@
         oh_cent[pl.ds(n * tile, n * tile), lanes] = hit
         oh_targ[:, lanes] = (node_row == targ_ref[s : s + 1, :] // LANES).astype(F32).astype(BF16)
         live = jnp.where(s < count, 1.0, 0.0).astype(F32)
-        hi, lo = split(maps_ref[s] * live)
+        hi, lo = split(maps[s] * live)
         maps2[s, pl.ds(0, LANES)] = hi.astype(BF16)
         maps2[s, pl.ds(LANES, LANES)] = lo.astype(BF16)
 
-    for d in offs:
-
-        @pl.when(there(d))
-        def _():
-            for c in setup_copies(-d, d):
-                c.wait_recv()
-            for c in setup_copies(d, -d):
-                c.wait_send()
-
-    vx[...] = vx[...] * gas
-    hx[...] = hx[...] * gas
     cell_row = iota((planes * rows, surf_here), 0)
-    for j in range(2 * reach + 1):
+
+    def hot_rows(j):
         oh_surf[j] = (cell_row == surf_all[j] // LANES).astype(F32).astype(BF16)
+
+    hot_rows(reach)
 
     lane_of = iota((LANES, surf_here), 0)
     group_of_slots = 4 if cap % 4 == 0 else 1
@@ -204,7 +265,7 @@
             c = src[z]
             dn = src[z - 1]
             lap = src[z + 1] + dn + in_plane(c) - 6.0 * c
-            dst[z] = c + cx[z] * lap - vx[z] * (c - dn) + hx[z] * jax.nn.sigmoid(2.0 * c)
+            dst[z] = c + cx[z] * lap - gas * vx[z] * (c - dn) + gas * hx[z] * jax.nn.sigmoid(2.0 * c)
 
     def as_row(t8):
         return jnp.concatenate([t8[i : i + 1, :] for i in range(half)], axis=1)
@@ -251,10 +312,13 @@
     def couple(it, carry):
         par = lax.rem(it, 2)
         last = it == COUPLE - 1
-        pair = (fa, fb)
-        for k in range(STEPS):
-            step(pair[k % 2], pair[(k + 1) % 2], k)
-        final = pair[STEPS % 2]
+        first = it == 0
+        final = fa
+
+        @pl.when(jnp.logical_not(first))
+        def _():
+            for k in range(STEPS):
+                step(pair[k % 2], pair[(k + 1) % 2], k)
 
         temp = jnp.concatenate([final[depth + p].T for p in range(planes)], axis=1)
         flux = jnp.concatenate(
@@ -329,13 +393,20 @@
         part[...] = jnp.where(q_of_row, p1, p0).reshape(n, tile, LANES)
         for k in range(1, n):
             rs_copy(k, me).start()
+
+        @pl.when(first)
+        def _():
+            each(offs, lambda d: starts(rest_copies(d, (2,))))
+
         rs_land[me] = part[me]
         for k in range(1, n):
             rs_copy(k, lax.rem(me + n - k, n)).wait_recv()
         iface = rs_land[0]
         for j in range(1, n):
             iface = iface + rs_land[j]
-        iface_ref[...] = iface
+        for q in range(2):
+            for i in range(half):
+                iface_ref[0, q : q + 1, i * LANES : (i + 1) * LANES] = iface[q * half + i : q * half + i + 1, :]
         inc = gain_t * (iface - exp_buf[...]) + pltpu.roll(gain_f * iface, half, 0)
         inc_buf[...] = inc
         for d in offs:
@@ -345,7 +416,18 @@
                 inc_copy(d, -d).start()
                 halo_copy(par, d, -d).wait_send()
 
+        @pl.when(first)
+        def _():
+            each(offs, lambda d: arrivals(surf_copies(-d)))
+            for d in offs:
+                hot_rows(d + reach)
+
         fa[own] = final[own] + spread(reach, inc)
+
+        @pl.when(first)
+        def _():
+            each(offs, lambda d: arrivals(rest_copies(-d, (0, 1, 2))))
+            each(offs, lambda d: departures(rest_copies(d, (0, 1, 2)) + surf_copies(d)))
 
         @pl.when(jnp.logical_not(last))
         def _():
@@ -370,8 +452,32 @@
             rs_copy(k, me).wait_send()
         return carry
 
+    pair = (fa, fb)
+    each(beside, lambda d: arrivals(first_copies(-d)))
+    each(beside, lambda d: departures(first_copies(d)))
+    for k in range(near):
+        step(pair[k % 2], pair[(k + 1) % 2], depth - near + k)
+    each(beside, lambda d: mid_copy(d).start())
+    each(offs, lambda d: starts(surf_copies(d) + rest_copies(d, (0, 1))))
+    each(beside, lambda d: mid_copy(-d).wait_recv())
+    for d in beside:
+        fa[pl.ds(depth + planes * d, planes)] = land[1, at[d]]
+    each(beside, lambda d: mid_copy(d).wait_send())
+    for k in range(near):
+        step(pair[k % 2], pair[(k + 1) % 2], depth - near + k)
+
     lax.fori_loop(0, COUPLE, couple, 0)
-    out_ref[...] = fa[own]
+
+    def fold(b, carry):
+        chunk = pl.ds(pl.multiple_of(b * 8 * LANES, LANES), 8 * LANES)
+        rws = []
+        for p in range(planes):
+            x = fa[depth + p, pl.ds(pl.multiple_of(b * 8, 8), 8), :]
+            rws.append(jnp.concatenate([x[i : i + 1, :] for i in range(8)], axis=1))
+        out_ref[0, :, chunk] = jnp.concatenate(rws, axis=0)
+        return carry
+
+    lax.fori_loop(0, rows // 8, fold, 0)
 
 
 def local_of(n, groups):
@@ -390,7 +496,6 @@
     ):
         _, planes, cells = initial_field.shape
         rows = cells // LANES
-        slab = (planes, rows, LANES)
         surf_here = surface_cell.shape[1]
         cap = patch_centres.shape[1]
         reach = -(-STEPS // planes)
@@ -420,8 +525,8 @@
             pltpu.VMEM((n, tile, LANES), F32),
             pltpu.VMEM((tile, LANES), F32),
             pltpu.VMEM((nd, tile, LANES), F32),
-            dma((5, nd)),
-            dma((5, nd)),
+            dma((9, nd)),
+            dma((9, nd)),
             dma((2, groups - 1)),
             dma((2, groups - 1)),
             dma((n - 1,)),
@@ -432,6 +537,8 @@
             dma((nd,)),
             dma((2, nd)),
             dma((2, nd)),
+            pltpu.VMEM((cap, LANES, LANES), F32),
+            dma(()),
         ]
 
         def body(*refs):
@@ -441,10 +548,10 @@
             body,
             name="coupled",
             out_shape=(
-                jax.ShapeDtypeStruct(slab, F32),
-                jax.ShapeDtypeStruct((tile, LANES), F32),
+                jax.ShapeDtypeStruct(initial_field.shape, F32),
+                jax.ShapeDtypeStruct((1, 2, surf_here), F32),
             ),
-            in_specs=[smem] * 3 + [vmem] * 8,
+            in_specs=[smem] * 3 + [vmem] * 7 + [pl.BlockSpec(memory_space=pl.ANY)],
             out_specs=(vmem, vmem),
             scratch_shapes=scratch,
             compiler_params=pltpu.CompilerParams(
@@ -454,16 +561,16 @@
             group_kind,
             partner,
             patch_count,
-            initial_field.reshape(slab),
-            conduct.reshape(slab),
-            velocity.reshape(slab),
-            heat_release.reshape(slab),
+            initial_field,
+            conduct,
+            velocity,
+            heat_release,
             surface_cell,
             patch_centres[0],
             patch_targets[0],
             patch_maps[0],
         )
-        return field.reshape(initial_field.shape), iface.reshape(1, 2, surf_here)
+        return field, iface
 
     return local
 

time: 101 us -> 92.9 us (0.920)
  Pallas kernels: 93.9 us -> 89.2 us
  local copies, waits for them, and re-layouts: 6.28 us -> 2.85 us
    reshape x4 -> x0, local copies, waits for them, and re-layouts: 6.28 us -> none  [the longest x2 2.91 us: local(): return (field.reshape(initial_field.shape), iface.reshape(1, 2, surf_here))]
    pallas_call x1, Pallas kernels: 93.9 us -> 89.2 us  [local(): pl.pallas_call(body, name='coupled', out_shape=(jax.ShapeDtypeStruct(init...]
    unnamed x0 -> x2, local copies, waits for them, and re-layouts: none -> 2.85 us
where the time goes in v2:
time: 92.9 us; the launch traced here: 92.7 us
  Pallas kernels  89.2 us (96%)
  local copies, waits for them, and re-layouts  2.85 us (3%)
    pallas_call x1, Pallas kernels, local(): pl.pallas_call(body, name='coupled', out_shape=(jax.ShapeDtypeStruct(init...  89.2 us
    unnamed x2, local copies, waits for them, and re-layouts  2.85 us

profile of v2, /device:TPU:0, one launch (start us, length us, event | category | flops | bytes accessed | tf_op | source)
XLA Modules:
  0.0 92.7 jit_solution(12959443832614185185)
XLA Ops:
  0.6 89.2 %coupled.1 = (f32[1,2,16384]{2,1,0:T(2,128)}, f32[1,2,512]{2,1,0:T(2,128)}) custom-call(s32[4]{0:T(128)} %refs_0_.1, s32[4]{0:T(128)} %refs_1_.1, s32[1,8]{1,0:T(1,128)} %refs_2_.1, f32[1,2,16384]{2,1,0:T(2,128)} %refs_3_.1, f32[1,2,16384]{2,1,0:T(2,128)} %refs_4_.1, f32[1,2,16384]{2,1,0:T(2,128)} %refs_5_.1, f32[1,2,16384]{2,1,0:T(2,128)} %refs_6_.1, ...), custom_call_target="tpu_custom_call" | custom-call | tf_op jit(solution)/shard_map/coupled/pallas_call | solution.py:547
  89.8 1.6 %copy.15 = f32[1,2,16384]{2,1,0:T(2,128)} copy(f32[1,2,16384]{2,1,0:T(2,128)} %get-tuple-element.4) | data formatting | bytes 262144
  91.4 1.3 %copy.16 = f32[1,2,512]{2,1,0:T(2,128)} copy(f32[1,2,512]{2,1,0:T(2,128)} %get-tuple-element.5) | data formatting | bytes 8192
